TPU v7x, 32 devices: a whole 2x2x4 slice. The times are simulated.
32 devices in a mesh: dp: 16 (over z, y, x), tensor: 2 (over core).
Axes of the slice: x: 2, y: 2, z: 4, core: 2. Of those that a mesh axis runs over, the one named last changes fastest.
Arguments:
- block_input: bfloat16 [4096, 1536], P('dp'), may hold values from -6 to 6
- norm_gain: float32 [2, 1536], replicated, may hold values from 0.5 to 1.5
- zx_weight: bfloat16 [2, 1536, 2, 3072], P(None, None, None, 'tensor'), may hold values from -0.15625 to 0.15625
- bc_weight: bfloat16 [2, 1536, 256], replicated, may hold values from -0.15625 to 0.15625
- dt_weight: bfloat16 [2, 1536, 48], P(None, None, 'tensor'), may hold values from -0.15625 to 0.15625
- conv_x: float32 [2, 5, 3072], P(None, None, 'tensor'), may hold values from -0.5 to 0.5
- conv_bc: float32 [2, 5, 256], replicated, may hold values from -0.5 to 0.5
- head_params: float32 [2, 3, 48], P(None, None, 'tensor'), may hold values from -7 to 2
- gate_gain: float32 [2, 3072], P(None, 'tensor'), may hold values from 0.5 to 1.5
- out_weight: bfloat16 [2, 3072, 1536], P(None, 'tensor'), may hold values from -0.109375 to 0.109375
- seq_lengths: int32 [4], replicated, may hold values from 1 to 2176, 4096 in all
- out_cotangent: bfloat16 [4096, 1536], P('dp'), may hold values from -6 to 6
Outputs:
- block_output: bfloat16 [4096, 1536], P('dp')
- input_grad: float32 [4096, 1536], P('dp')
- norm_gain_grad: float32 [2, 1536], replicated
- zx_weight_grad: float32 [2, 1536, 2, 3072], P(None, 'dp', None, 'tensor')
- bc_weight_grad: float32 [2, 1536, 256], P(None, 'dp')
- dt_weight_grad: float32 [2, 1536, 48], P(None, 'dp', 'tensor')
- conv_x_grad: float32 [2, 5, 3072], P(None, None, 'tensor')
- conv_bc_grad: float32 [2, 5, 256], replicated
- head_params_grad: float32 [2, 3, 48], P(None, None, 'tensor')
- gate_gain_grad: float32 [2, 3072], P(None, 'tensor')
- out_weight_grad: float32 [2, 3072, 1536], P(None, 'tensor', 'dp')
Inputs may be any that keep to these rules, and one draw needn't show every extreme that they name: `seq_lengths`: the lengths sum to 4096 and the longest is exactly 2176.
All inputs are finite; a program needn't handle non-finite values.
Results may differ from a plain program's by a relative error of at most 0.012.
The roundings to bfloat16 on the way count: a program that leaves them out, or rounds other values in their place, can miss the bound.
Values sent between devices are 32-bit elements; how exact they have to be, the bound alone decides.
A program may use at most 320 MiB of HBM per device.

v0:
```python
import jax
import jax.numpy as jnp
from jax import lax
from jax.sharding import PartitionSpec as P

D = 1536
CONV = 4
GROUP = 256
LAYERS = 2
INNER = 3072


epsilon = 1e-05


def shifted(array, axis, by):
    size = lax.axis_size(axis)
    pairs = [(i, i + by) for i in range(size) if 0 <= i + by < size]
    return lax.ppermute(array, axis, pairs)


def entering(array, axis, combine, identity, reverse):
    size, place = (lax.axis_size(axis), lax.axis_index(axis))
    everything = jax.tree.map(lambda part: lax.all_gather(part, axis), array)
    start = jax.tree.map(
        lambda part, zero: jnp.broadcast_to(jnp.asarray(zero, part.dtype), part.shape),
        array,
        identity,
    )

    def hop(k, before):
        at = size - 1 - k if reverse else k
        reached = at > place if reverse else at < place
        new = combine(before, jax.tree.map(lambda part: part[at], everything))
        return jax.tree.map(lambda a, b: jnp.where(reached, a, b), new, before)

    return lax.fori_loop(0, size, hop, start)


def segment_of(positions, seq_ends):
    counted = jnp.sum((seq_ends[None, :] <= positions[:, None]).astype(jnp.int32), axis=1)
    return jnp.where(positions < 0, -1, counted)


def rms_scale(hidden, gain):
    mean_sq = jnp.mean(hidden * hidden, axis=1, keepdims=True)
    return hidden * lax.rsqrt(mean_sq + epsilon) * gain


def conv_silu(pre_ext, seg_ext, tap_rows):
    count = pre_ext.shape[0] - (CONV - 1)
    current = seg_ext[CONV - 1 :]
    total = jnp.zeros((count, pre_ext.shape[1]), jnp.float32) + tap_rows[CONV]
    for offset in range(CONV):
        same_seq = seg_ext[offset : offset + count] == current
        total = total + tap_rows[offset] * jnp.where(
            same_seq[:, None], pre_ext[offset : offset + count], 0.0
        )
    return jax.nn.silu(total)


def group_step(state_now, group_inputs):
    x_scaled, rate_block, b_block, c_block, seg_block, seg_prior = group_inputs
    cumulative = jnp.cumsum(rate_block, axis=0)
    length = seg_block.shape[0]
    lower_mask = jnp.arange(length)[:, None] >= jnp.arange(length)[None, :]
    same_mask = lower_mask & (seg_block[:, None] == seg_block[None, :])
    decayed = jnp.exp(
        jnp.where(same_mask[:, :, None], cumulative[:, None, :] - cumulative[None, :, :], -1e30)
    )
    intersection = jnp.dot(c_block, b_block.T, precision=lax.Precision.HIGHEST)
    outputs = jnp.einsum(
        "ijh,jhp->ihp",
        decayed * intersection[:, :, None],
        x_scaled,
        precision=lax.Precision.HIGHEST,
    )
    alive_rows = (seg_block == seg_prior).astype(jnp.float32)
    carried = jnp.einsum("in,hpn->ihp", c_block, state_now, precision=lax.Precision.HIGHEST)
    outputs = outputs + (alive_rows[:, None] * jnp.exp(cumulative))[:, :, None] * carried
    to_end = jnp.where(
        (seg_block == seg_block[-1])[:, None], jnp.exp(cumulative[-1][None, :] - cumulative), 0.0
    )
    state_next = (alive_rows[-1] * jnp.exp(cumulative[-1]))[:, None, None] * state_now
    state_next = state_next + jnp.einsum(
        "jh,jhp,jn->hpn", to_end, x_scaled, b_block, precision=lax.Precision.HIGHEST
    )
    return (state_next, outputs)


def local_scan(x_act, dt_raw, bc_act, params, segments, seg_before, start_state):
    count = x_act.shape[0]
    heads = params.shape[1]
    width = x_act.shape[1] // heads
    half = bc_act.shape[1] // 2
    step_size = jax.nn.softplus(dt_raw + params[0])
    rate = -jnp.exp(params[1]) * step_size
    x_heads = x_act.reshape(count, heads, width)
    x_scaled = x_heads * step_size[:, :, None]
    blocks = count // GROUP
    group_inputs = (
        x_scaled.reshape(blocks, GROUP, heads, width),
        rate.reshape(blocks, GROUP, heads),
        bc_act[:, :half].reshape(blocks, GROUP, half),
        bc_act[:, half:].reshape(blocks, GROUP, half),
        segments.reshape(blocks, GROUP),
        seg_before,
    )
    final_state, outputs = lax.scan(group_step, start_state, group_inputs)
    return (
        outputs.reshape(count, heads, width) + params[2][None, :, None] * x_heads,
        final_state,
        rate,
    )


def device_section(x_act, dt_raw, bc_act, params, segments, seg_before, seg_prior):
    heads = params.shape[1]
    half = bc_act.shape[1] // 2
    start_state = jnp.zeros((heads, x_act.shape[1] // heads, half), jnp.float32)
    outputs, final_state, rate = local_scan(
        x_act, dt_raw, bc_act, params, segments, seg_before, start_state
    )
    cumulative = jnp.cumsum(rate, axis=0)
    through = (segments[-1] == seg_prior).astype(jnp.float32)
    return (outputs, final_state, through * jnp.exp(cumulative[-1]), cumulative, bc_act[:, half:])


def state_input(incoming, cumulative, c_matrix, alive_rows):
    weights = alive_rows[:, None] * jnp.exp(cumulative)
    return weights[:, :, None] * jnp.einsum(
        "tn,hpn->thp", c_matrix, incoming, precision=lax.Precision.HIGHEST
    )


def chain(earlier, later):
    return (earlier[0] * later[0], later[0][:, None, None] * earlier[1] + later[1])


def contract_rows(left, right):
    return lax.dot_general(
        left, right, (((0,), (0,)), ((), ())), preferred_element_type=jnp.float32
    )


def contract_cols(left, right):
    return lax.dot_general(
        left, right, (((1,), (1,)), ((), ())), preferred_element_type=jnp.float32
    )


def per_device(
    block_input,
    norm_gain,
    zx_weight,
    bc_weight,
    dt_weight,
    conv_x,
    conv_bc,
    head_params,
    gate_gain,
    out_weight,
    seq_lengths,
    out_cotangent,
):
    token_rows = block_input.shape[0]
    inner_local = out_weight.shape[1]
    heads_local = head_params.shape[2]
    tail_rows = CONV - 1
    split_at = token_rows - tail_rows
    seq_ends = jnp.cumsum(seq_lengths)
    first_pos = lax.axis_index("dp") * token_rows
    segments = segment_of(first_pos + jnp.arange(token_rows, dtype=jnp.int32), seq_ends)
    seg_ext = segment_of(first_pos + jnp.arange(-tail_rows, token_rows, dtype=jnp.int32), seq_ends)
    seg_before = segment_of(
        first_pos + jnp.arange(token_rows // GROUP, dtype=jnp.int32) * GROUP - 1, seq_ends
    )
    seg_prior = seg_before[0]
    alive_rows = (segments == seg_prior).astype(jnp.float32)

    def section_fn(x_act, dt_raw, bc_act, params):
        return device_section(x_act, dt_raw, bc_act, params, segments, seg_before, seg_prior)

    def state_fn(incoming, cumulative, c_matrix):
        return state_input(incoming, cumulative, c_matrix, alive_rows)

    def conv_fn(pre_ext, tap_rows):
        return conv_silu(pre_ext, seg_ext, tap_rows)

    hidden = block_input.astype(jnp.float32)
    kept = []
    for layer_index in range(LAYERS):
        w_zx = zx_weight[layer_index].reshape(D, 2 * inner_local)
        normed_f, pull_norm = jax.vjp(rms_scale, hidden, norm_gain[layer_index])
        normed_bf = normed_f.astype(jnp.bfloat16)
        projected = jnp.dot(normed_bf, w_zx, preferred_element_type=jnp.float32)
        gate_in = projected[:, :inner_local]
        x_pre = projected[:, inner_local:]
        bc_pre = jnp.dot(normed_bf, bc_weight[layer_index], preferred_element_type=jnp.float32)
        dt_raw = jnp.dot(normed_bf, dt_weight[layer_index], preferred_element_type=jnp.float32)
        tails = shifted((x_pre[split_at:], bc_pre[split_at:]), "dp", 1)
        x_ext = jnp.concatenate([tails[0], x_pre], 0)
        bc_ext = jnp.concatenate([tails[1], bc_pre], 0)
        x_act, pull_cx = jax.vjp(conv_fn, x_ext, conv_x[layer_index])
        bc_act, pull_cbc = jax.vjp(conv_fn, bc_ext, conv_bc[layer_index])
        section_out, pull_section = jax.vjp(
            section_fn, x_act, dt_raw, bc_act, head_params[layer_index]
        )
        outputs, final_state, through, cumulative, c_matrix = section_out
        prefix = entering(
            (through, final_state),
            "dp",
            chain,
            (jnp.ones_like(through), jnp.zeros_like(final_state)),
            False,
        )
        incoming = prefix[1]
        from_state, pull_state = jax.vjp(state_fn, incoming, cumulative, c_matrix)
        ssd_out = (outputs + from_state).reshape(token_rows, inner_local)
        gated = ssd_out * jax.nn.silu(gate_in)
        squares = lax.psum(jnp.sum(gated * gated, axis=1), "tensor")
        scale = lax.rsqrt(squares / INNER + epsilon)
        mixed = (gated * scale[:, None] * gate_gain[layer_index]).astype(jnp.bfloat16)
        out_sum = lax.psum(
            jnp.dot(mixed, out_weight[layer_index], preferred_element_type=jnp.float32), "tensor"
        )
        kept.append(
            (
                pull_norm,
                normed_bf,
                gate_in,
                ssd_out,
                gated,
                scale,
                mixed,
                pull_cx,
                pull_cbc,
                pull_section,
                pull_state,
                incoming,
                through,
            )
        )
        hidden = hidden + out_sum
    block_output = hidden.astype(jnp.bfloat16)
    grad = out_cotangent.astype(jnp.float32)
    large_list = []
    small_list = []
    for layer_index in reversed(range(LAYERS)):
        (
            pull_norm,
            normed_bf,
            gate_in,
            ssd_out,
            gated,
            scale,
            mixed,
            pull_cx,
            pull_cbc,
            pull_section,
            pull_state,
            incoming,
            through,
        ) = kept[layer_index]
        grad_bf = grad.astype(jnp.bfloat16)
        d_out_w = contract_rows(mixed, grad_bf)
        d_mixed = contract_cols(grad_bf, out_weight[layer_index])
        gain_row = gate_gain[layer_index]
        d_gate_gain = jnp.sum(d_mixed * gated * scale[:, None], axis=0)
        dotted = lax.psum(jnp.sum(d_mixed * gain_row * gated, axis=1), "tensor")
        d_gated = (
            scale[:, None] * gain_row * d_mixed
            - gated * (scale * scale * scale * dotted / INNER)[:, None]
        )
        sigma = jax.nn.sigmoid(gate_in)
        d_ssd = d_gated * gate_in * sigma
        d_z = d_gated * ssd_out * sigma * (1.0 + gate_in * (1.0 - sigma))
        d_heads = d_ssd.reshape(token_rows, heads_local, -1)
        d_incoming, d_cumul, d_cmatrix = pull_state(d_heads)
        later = entering(
            (through, d_incoming),
            "dp",
            chain,
            (jnp.ones_like(through), jnp.zeros_like(d_incoming)),
            True,
        )
        d_final = later[1]
        d_through = jnp.sum(d_final * incoming, axis=(1, 2))
        d_xact, d_dtraw, d_bcact, d_params = pull_section(
            (d_heads, d_final, d_through, d_cumul, d_cmatrix)
        )
        d_bcact = lax.psum(d_bcact, "tensor")
        d_xext, d_cx = pull_cx(d_xact)
        d_bcext, d_cbc = pull_cbc(d_bcact)
        back = shifted((d_xext[:tail_rows], d_bcext[:tail_rows]), "dp", -1)
        d_xcore = d_xext[tail_rows:]
        d_bccore = d_bcext[tail_rows:]
        d_xpre = jnp.concatenate([d_xcore[:split_at], d_xcore[split_at:] + back[0]], 0)
        d_bcpre = jnp.concatenate([d_bccore[:split_at], d_bccore[split_at:] + back[1]], 0)
        d_proj = jnp.concatenate([d_z, d_xpre], 1).astype(jnp.bfloat16)
        d_bc_bf = d_bcpre.astype(jnp.bfloat16)
        d_dt_bf = d_dtraw.astype(jnp.bfloat16)
        w_zx = zx_weight[layer_index].reshape(D, 2 * inner_local)
        d_zx_w = contract_rows(normed_bf, d_proj).reshape(D, 2, inner_local)
        d_bc_w = contract_rows(normed_bf, d_bc_bf)
        d_dt_w = contract_rows(normed_bf, d_dt_bf)
        head_part = contract_cols(d_proj, w_zx) + contract_cols(d_dt_bf, dt_weight[layer_index])
        d_normed = lax.psum(head_part, "tensor") + contract_cols(d_bc_bf, bc_weight[layer_index])
        d_hidden, d_norm_gain = pull_norm(d_normed)
        grad = grad + d_hidden
        large_list.insert(0, (d_zx_w, d_bc_w, d_dt_w, d_out_w))
        small_list.insert(0, (d_norm_gain, d_cx, d_cbc, d_params, d_gate_gain))
    large_stack = tuple((jnp.stack([entry[slot] for entry in large_list], 0) for slot in range(4)))
    small_stack = tuple((jnp.stack([entry[slot] for entry in small_list], 0) for slot in range(5)))
    large_sums = (
        lax.psum_scatter(large_stack[0], "dp", scatter_dimension=1, tiled=True),
        lax.psum_scatter(large_stack[1], "dp", scatter_dimension=1, tiled=True),
        lax.psum_scatter(large_stack[2], "dp", scatter_dimension=1, tiled=True),
        lax.psum_scatter(large_stack[3], "dp", scatter_dimension=2, tiled=True),
    )
    small_sums = lax.psum(
        (small_stack[0], small_stack[1], small_stack[2], small_stack[3], small_stack[4]), "dp"
    )
    return (
        block_output,
        grad,
        small_sums[0],
        large_sums[0],
        large_sums[1],
        large_sums[2],
        small_sums[1],
        small_sums[2],
        small_sums[3],
        small_sums[4],
        large_sums[3],
    )


def solution(mesh):
    placed = (
        P("dp", None),
        P(),
        P(None, None, None, "tensor"),
        P(),
        P(None, None, "tensor"),
        P(None, None, "tensor"),
        P(),
        P(None, None, "tensor"),
        P(None, "tensor"),
        P(None, "tensor", None),
        P(),
        P("dp", None),
    )
    return jax.shard_map(
        per_device,
        mesh=mesh,
        in_specs=placed,
        out_specs=(
            P("dp", None),
            P("dp", None),
            P(),
            P(None, "dp", None, "tensor"),
            P(None, "dp", None),
            P(None, "dp", "tensor"),
            P(None, None, "tensor"),
            P(),
            P(None, None, "tensor"),
            P(None, "tensor"),
            P(None, "tensor", "dp"),
        ),
        check_vma=False,
    )
```

profile of v0, /device:TPU:0, one launch (start us, length us, event | category | flops | bytes accessed | tf_op | source)
XLA Modules:
  0.0 2553.3 jit_solution(9537686367697434273)
XLA Ops:
  16.2 15.8 fusion.313
  32.0 9.8 copy.213
  71.5 40.2 %all-gather.4 = f32[16,1,24]{2,1,0:T(1,128)} all-gather(f32[1,1,24]{2,1,0:T(1,128)S(1)} %bitcast.538), channel_id=1, replica_groups=mesh['dp'=16,'tensor'=2] {'dp'}, dimensions={0}, use_global_device_ids=true | all-gather | bytes 1632 | tf_op jit(solution)/shard_map/all_gather | solution.py:24
  118.2 105.2 %all-gather.11.cloned.1.call-done = f32[384,64,128]{2,1,0:T(8,128)} async-done(((f32[24,64,128]{2,1,0:T(8,128)}), f32[384,64,128]{2,1,0:T(8,128)}) %all-gather.11.cloned.1.call-update) | async-done | bytes 12582928 | tf_op jit(solution)/shard_map/all_gather | solution.py:24
  223.4 32.1 %while.40 = (s32[]{:T(128)}, f32[24,64,128]{2,1,0:T(8,128)S(1)}, s32[]{:T(128)}, f32[16,24]{1,0:T(8,128)}, f32[16,24,64,128]{3,2,1,0:T(8,128)}, /*index=5*/s32[]{:T(128)}, s32[]{:T(128)}) while((s32[]{:T(128)}, f32[24,64,128]{2,1,0:T(8,128)S(1)}, s32[]{:T(128)}, f32[16,24]{1,0:T(8,128)}, f32[16,24,64,128]{3,2,1,0:T(8,128)}, ...), condition=%wide.region_8.10_spmd.clone, body=%wide.region_7.9_spmd.clone.sunk | while | flops 786436 | bytes 2359697 | solution.py:37
  257.0 8.2 fusion.81
  278.1 9.8 copy.214
  288.0 8.8 all-reduce.64.cloned.1.call-done
  327.3 42.1 %all-gather.5 = f32[16,1,24]{2,1,0:T(1,128)} all-gather(f32[1,1,24]{2,1,0:T(1,128)S(1)} %bitcast.537), channel_id=1, replica_groups=mesh['dp'=16,'tensor'=2] {'dp'}, dimensions={0}, use_global_device_ids=true | all-gather | bytes 1632 | tf_op jit(solution)/shard_map/all_gather | solution.py:24
  372.3 108.3 %all-gather.13.cloned.1.call-done = f32[384,64,128]{2,1,0:T(8,128)} async-done(((f32[24,64,128]{2,1,0:T(8,128)}), f32[384,64,128]{2,1,0:T(8,128)}) %all-gather.13.cloned.1.call-update) | async-done | bytes 12582928 | tf_op jit(solution)/shard_map/all_gather | solution.py:24
  480.6 32.2 %while.41 = (s32[]{:T(128)}, f32[24,64,128]{2,1,0:T(8,128)S(1)}, s32[]{:T(128)}, f32[16,24]{1,0:T(8,128)}, f32[16,24,64,128]{3,2,1,0:T(8,128)}, /*index=5*/s32[]{:T(128)}, s32[]{:T(128)}) while((s32[]{:T(128)}, f32[24,64,128]{2,1,0:T(8,128)S(1)}, s32[]{:T(128)}, f32[16,24]{1,0:T(8,128)}, f32[16,24,64,128]{3,2,1,0:T(8,128)}, ...), condition=%wide.region_16.18_spmd.clone, body=%wide.region_15.17_spmd.clone.sunk | while | flops 786436 | bytes 2359697 | solution.py:37
  514.2 9.6 fusion.79
  561.9 10.0 fusion.33
  573.0 131.8 %all-gather.15.cloned.1.call-done = f32[384,64,128]{2,1,0:T(8,128)} async-done(((f32[24,64,128]{2,1,0:T(8,128)}), f32[384,64,128]{2,1,0:T(8,128)}) %all-gather.15.cloned.1.call-update) | async-done | bytes 12582928 | tf_op jit(solution)/shard_map/all_gather | solution.py:24
  704.8 32.2 %while.42 = (s32[]{:T(128)}, f32[24,64,128]{2,1,0:T(8,128)S(1)}, s32[]{:T(128)}, f32[16,24]{1,0:T(8,128)}, f32[16,24,64,128]{3,2,1,0:T(8,128)}, /*index=5*/s32[]{:T(128)}, s32[]{:T(128)}, s32[]{:T(128)}, s32[]{:T(128)}) while((s32[]{:T(128)}, f32[24,64,128]{2,1,0:T(8,128)S(1)}, s32[]{:T(128)}, f32[16,24]{1,0:T(8,128)}, ...), condition=%wide.region_23.25_spmd.clone, body=%wide.region_22.24_spmd.clone.sunk | while | flops 786440 | bytes 2359759 | solution.py:37
  743.2 8.3 multiply_reduce_fusion.1
  787.4 21.3 all-reduce.72.cloned.1.call-done
  850.1 10.0 fusion.35
  861.8 130.6 %all-gather.17.cloned.1.call-done = f32[384,64,128]{2,1,0:T(8,128)} async-done(((f32[24,64,128]{2,1,0:T(8,128)}), f32[384,64,128]{2,1,0:T(8,128)}) %all-gather.17.cloned.1.call-update) | async-done | bytes 12582928 | tf_op jit(solution)/shard_map/all_gather | solution.py:24
  992.4 32.2 %while.43 = (s32[]{:T(128)}, f32[24,64,128]{2,1,0:T(8,128)S(1)}, s32[]{:T(128)}, f32[16,24]{1,0:T(8,128)}, f32[16,24,64,128]{3,2,1,0:T(8,128)}, /*index=5*/s32[]{:T(128)}, s32[]{:T(128)}, s32[]{:T(128)}, s32[]{:T(128)}) while((s32[]{:T(128)}, f32[24,64,128]{2,1,0:T(8,128)S(1)}, s32[]{:T(128)}, f32[16,24]{1,0:T(8,128)}, ...), condition=%wide.region_43.45_spmd.clone, body=%wide.region_42.44_spmd.clone.sunk | while | flops 786440 | bytes 2359759 | solution.py:37
  1090.9 28.7 %copy.186 = f32[2,1536,1536]{1,0,2:T(2,128)} copy(f32[2,1536,1536]{2,1,0:T(8,128)} %pad_maximum_fusion.1) | data formatting | bytes 37748736 | tf_op jit(solution)/shard_map/stack | solution.py:313
  1121.4 8.9 fusion.176
  1130.4 24.7 stack_reshape.7
  1164.1 8.3 fusion.174
  1172.5 24.7 stack_reshape.6
  1207.3 26.3 %copy_bitcast_fusion = f32[1536,2,2,1536]{3,2,1,0:T(2,128)} fusion(f32[1,1536,2,1536]{3,2,1,0:T(2,128)} %stack_reshape.7, f32[1,1536,2,1536]{3,2,1,0:T(2,128)} %stack_reshape.6), kind=kLoop, calls=%fused_computation.13 | loop fusion | flops 9437184 | bytes 75497472
  1233.6 46.5 %reshape.830 = f32[1536,6144]{1,0:T(8,128)} reshape(f32[1536,2,2,1536]{3,2,1,0:T(2,128)} %copy_bitcast_fusion) | data formatting | bytes 75497472
  1285.7 333.8 %all-reduce.66.cloned.1.call-done = f32[2,1536,1536]{1,0,2:T(2,128)} async-done(((f32[2,1536,1536]{1,0,2:T(2,128)}), f32[2,1536,1536]{1,0,2:T(2,128)}) %all-reduce.66.cloned.1.call-update) | async-done | bytes 18874384
  1622.0 125.5 %reduce-scatter.13.cloned.1.call-done = f32[96,48]{1,0:T(8,128)} async-done(((f32[1536,48]{1,0:T(8,128)}), f32[96,48]{1,0:T(8,128)}) %reduce-scatter.13.cloned.1.call-update) | async-done | bytes 18448
  1753.4 109.2 %all-reduce.68.cloned.1.call-done = (f32[2,1536]{1,0:T(2,128)}, f32[2,5,1536]{2,1,0:T(8,128)}, f32[2,5,256]{2,1,0:T(8,128)}, f32[2,3,24]{2,1,0:T(4,128)}, f32[2,1536]{1,0:T(2,128)}) async-done(((f32[2,1536]{1,0:T(2,128)}, f32[2,5,1536]{2,1,0:T(8,128)}, f32[2,5,256]{2,1,0:T(8,128)}, f32[2,3,24]{2,1,0:T(4,128)}, f32[2,1536]{1,0:T(2,128)}), (f32[2,1536]{1,0:T(2,128)}, f32[2,5,1536]{2,1,0:T(8,128)}, ...) | async-done | bytes 96848 | tf_op jit(solution)/shard_map/psum | solution.py:321
  1866.8 541.2 %reduce-scatter.11.cloned.1.call-done = f32[96,6144]{1,0:T(8,128)} async-done(((f32[1536,6144]{1,0:T(8,128)}), f32[96,6144]{1,0:T(8,128)}) %reduce-scatter.11.cloned.1.call-update) | async-done | bytes 2359312
  2413.5 131.4 %reduce-scatter.9.cloned.1.call-done = f32[2,96,256]{2,1,0:T(8,128)} async-done(((f32[2,1536,256]{2,1,0:T(8,128)}), f32[2,96,256]{2,1,0:T(8,128)}) %reduce-scatter.9.cloned.1.call-update) | async-done | bytes 196624 | tf_op jit(solution)/shard_map/reduce_scatter | solution.py:317
  (830 shorter events, 453.4 us)
Async XLA Ops:
  7.2 216.2 %all-gather.11.cloned.1.call-start = ((), (), s32[]{:S(2)}) async-start(), calls=%async_computation.5 | async-start | bytes 13369344 | tf_op jit(solution)/shard_map/all_gather | solution.py:24
  8.6 49.3 %copy-start.118 = (f32[256]{0:T(256)}, f32[256]{0:T(256)S(1)}, u32[]{:S(2)}) copy-start(f32[256]{0:T(256)S(1)} %fusion.279) | copy-start | bytes 3076
  9.4 48.4 %copy-start.69 = (f32[1536]{0:T(1024)}, f32[1536]{0:T(1024)S(1)}, u32[]{:S(2)}) copy-start(f32[1536]{0:T(1024)S(1)} %get-tuple-element.1007) | copy-start | bytes 18436
  11.3 51.8 %copy-start.62 = (f32[256,256]{1,0:T(8,128)}, f32[256,256]{1,0:T(8,128)S(1)}, u32[]{:S(2)}) copy-start(f32[256,256]{1,0:T(8,128)S(1)} %fusion.150) | copy-start | bytes 786436
  11.3 51.8 %collective-permute-start.1 = (f32[3,256]{1,0:T(4,128)S(1)}, f32[3,256]{1,0:T(4,128)S(1)}, u32[]{:S(2)}, u32[]{:S(2)}) collective-permute-start(f32[3,256]{1,0:T(4,128)S(1)} %slice.505), channel_id=1, source_target_pairs={{0,2},{2,4},{4,6},{6,8},{8,10},{10,12},{12,14},{14,16},{16,18},{18... | collective-permute-start | bytes 9224 | tf_op jit(solution)/shard_map/ppermute | solution.py:19
  48.8 15.5 collective-permute-start
  59.2 197.7 %copy-start.83 = (f32[256,24]{0,1:T(8,128)}, f32[256,24]{0,1:T(8,128)S(1)}, u32[]{:S(2)}) copy-start(f32[256,24]{0,1:T(8,128)S(1)} %bitcast_bitcast_fusion.3) | copy-start | bytes 73732
  69.1 187.8 %copy-start.20 = (f32[256,1536]{0,1:T(8,128)}, f32[256,1536]{0,1:T(8,128)S(1)}, u32[]{:S(2)}) copy-start(f32[256,1536]{0,1:T(8,128)S(1)} %copy.158) | copy-start | bytes 4718596
  71.4 225.3 %all-reduce.64.cloned.1.call-start = ((), (), s32[]{:S(2)}) async-start(), calls=%async_computation.3 | async-start | bytes 3145728 | tf_op jit(solution)/shard_map/psum | solution.py:224
  278.1 202.5 %all-gather.13.cloned.1.call-start = ((), (), s32[]{:S(2)}) async-start(), calls=%async_computation.6 | async-start | bytes 13369344 | tf_op jit(solution)/shard_map/all_gather | solution.py:24
  304.5 14.0 collective-permute-start.3
  315.2 4.9 collective-permute-start.2
  327.2 377.5 %all-gather.15.cloned.1.call-start = ((), (), s32[]{:S(2)}) async-start(), calls=%async_computation.7 | async-start | bytes 13369344 | tf_op jit(solution)/shard_map/all_gather | solution.py:24
  369.7 144.4 %copy-start.78 = (f32[256,256]{1,0:T(8,128)}, f32[256,256]{1,0:T(8,128)S(1)}, u32[]{:S(2)}) copy-start(f32[256,256]{1,0:T(8,128)S(1)} %fusion.220) | copy-start | bytes 786436
  555.0 253.7 %all-reduce.72.cloned.1.call-start = ((), (), s32[]{:S(2)}) async-start(), calls=%async_computation.14 | async-start | bytes 3670016 | tf_op jit(solution)/shard_map/psum | solution.py:308
  772.8 6.1 collective-permute-start.4
  787.3 205.1 %all-gather.17.cloned.1.call-start = ((), (), s32[]{:S(2)}) async-start(), calls=%async_computation.8 | async-start | bytes 13369344 | tf_op jit(solution)/shard_map/all_gather | solution.py:24
  810.8 5.8 collective-permute-start.5
  838.7 358.5 %all-reduce.70.cloned.1.call-start = ((), (), s32[]{:S(2)}) async-start(), calls=%async_computation.13 | async-start | bytes 6815744 | tf_op jit(solution)/shard_map/psum | solution.py:224
  1064.0 6.1 collective-permute-start.6
  1078.0 541.5 %all-reduce.66.cloned.1.call-start = ((), (), s32[]{:S(2)}) async-start(), calls=%async_computation.11 | async-start | bytes 37748736
  1119.8 627.8 %reduce-scatter.13.cloned.1.call-start = ((), (), s32[]{:S(2)}) async-start(), calls=%async_computation.10 | async-start | bytes 835584
  1164.0 698.6 %all-reduce.68.cloned.1.call-start = ((), (), s32[]{:S(2)}) async-start(), calls=%async_computation.12 | async-start | bytes 286720 | tf_op jit(solution)/shard_map/psum | solution.py:321
  1172.4 26.0 %copy-start.170 = (f32[1,1,256]{2,0,1:T(1,128)S(1)}, f32[1,1,256]{2,0,1:T(1,128)}, u32[]{:S(2)}) copy-start(f32[1,1,256]{2,0,1:T(1,128)} %copy-done.169) | copy-start | bytes 3076
  1172.4 26.0 %copy-start.172 = (f32[1,1,256]{2,0,1:T(1,128)S(1)}, f32[1,1,256]{2,0,1:T(1,128)}, u32[]{:S(2)}) copy-start(f32[1,1,256]{2,0,1:T(1,128)} %copy-done.171) | copy-start | bytes 3076
  1172.5 26.0 %copy-start.174 = (f32[1,1,256]{2,0,1:T(1,128)S(1)}, f32[1,1,256]{2,0,1:T(1,128)}, u32[]{:S(2)}) copy-start(f32[1,1,256]{2,0,1:T(1,128)} %copy-done.173) | copy-start | bytes 3076
  1198.8 6.0 collective-permute-start.7
  1207.3 1200.7 %reduce-scatter.11.cloned.1.call-start = ((), (), s32[]{:S(2)}) async-start(), calls=%async_computation.9 | async-start | bytes 40108032
  1280.2 1264.8 %reduce-scatter.9.cloned.1.call-start = ((), (), s32[]{:S(2)}) async-start(), calls=%async_computation.4 | async-start | bytes 3342336 | tf_op jit(solution)/shard_map/reduce_scatter | solution.py:317
  1620.8 128.4 %copy-start.2 = (f32[256,1536]{1,0:T(8,128)S(1)}, f32[256,1536]{1,0:T(8,128)}, u32[]{:S(2)}) copy-start(f32[256,1536]{1,0:T(8,128)} %copy-done) | copy-start | bytes 4718596
  2411.3 133.7 %copy-start.159 = (f32[2,1536]{1,0:T(2,128)S(1)}, f32[2,1536]{1,0:T(2,128)}, u32[]{:S(2)}) copy-start(f32[2,1536]{1,0:T(2,128)} %get-tuple-element.1385) | copy-start | bytes 36868
  2411.3 134.3 %copy-start.158 = (f32[2,1536]{1,0:T(2,128)S(1)}, f32[2,1536]{1,0:T(2,128)}, u32[]{:S(2)}) copy-start(f32[2,1536]{1,0:T(2,128)} %get-tuple-element.1392) | copy-start | bytes 36868
  (199 other events, 1366.2 us)
Sparse Core Ops, SparseCore 0:
  71.6 151.7 all-gather.10
  278.2 18.5 all-reduce.63
  327.3 153.1 all-gather.12
  555.1 149.5 all-gather.14
  787.4 21.1 all-reduce.71
  838.8 153.5 all-gather.16
  1078.1 24.2 all-reduce.69
  1119.9 499.5 all-reduce.65
  1624.7 122.7 reduce-scatter.12
  1754.6 107.9 all-reduce.67
  1868.6 539.2 reduce-scatter.10
  2413.4 131.5 reduce-scatter.8
where the time goes:
time: 2570 us; the launch traced here: 2550 us
  waiting for transfers between devices  1760 us (68%)
  local copies, waits for them, and re-layouts  274 us (11%)
  other arithmetic  209 us (8%)
  matrix products  179 us (7%)
  blocking collectives  92.4 us (4%)
    unnamed x15, waiting for transfers between devices  1000 us
    all_gather x4, waiting for transfers between devices, entering(): everything = jax.tree.map(lambda part: lax.all_gather(part, axis), array)  476 us
    reduce_scatter x1, waiting for transfers between devices, per_device(): lax.psum_scatter(large_stack[1], 'dp', scatter_dimension=1, tiled=True)  131 us
    psum x1, waiting for transfers between devices, per_device(): lax.psum((small_stack[0], small_stack[1], small_stack[2], small_stack[3],...  109 us
    unnamed x439, local copies, waits for them, and re-layouts  101 us
    select_n x64, other arithmetic, hop(): return jax.tree.map(lambda a, b: jnp.where(reached, a, b), new, before)  83.1 us
    all_gather x2, blocking collectives, entering(): everything = jax.tree.map(lambda part: lax.all_gather(part, axis), array)  82.2 us
    another operation x3, local copies, waits for them, and re-layouts, per_device(): jnp.stack([entry[slot] for entry in large_list], 0)  78 us
  transfers between devices with their start and end apart: 20, of which 16 were waited for; matrix products, arithmetic and copies ran while one was open for 13% of the time, Pallas kernels for 0%

commit v1 on v0

--- a/solution.py
+++ b/solution.py
@@ -1,6 +1,10 @@
+import functools
+
 import jax
 import jax.numpy as jnp
 from jax import lax
+from jax.experimental import pallas as pl
+from jax.experimental.pallas import tpu as pltpu
 from jax.sharding import PartitionSpec as P
 
 D = 1536
@@ -8,6 +12,7 @@
 GROUP = 256
 LAYERS = 2
 INNER = 3072
+PLANE = 4
 
 
 epsilon = 1e-05
@@ -19,22 +24,145 @@
     return lax.ppermute(array, axis, pairs)
 
 
-def entering(array, axis, combine, identity, reverse):
-    size, place = (lax.axis_size(axis), lax.axis_index(axis))
-    everything = jax.tree.map(lambda part: lax.all_gather(part, axis), array)
-    start = jax.tree.map(
-        lambda part, zero: jnp.broadcast_to(jnp.asarray(zero, part.dtype), part.shape),
-        array,
-        identity,
-    )
-
-    def hop(k, before):
-        at = size - 1 - k if reverse else k
-        reached = at > place if reverse else at < place
-        new = combine(before, jax.tree.map(lambda part: part[at], everything))
-        return jax.tree.map(lambda a, b: jnp.where(reached, a, b), new, before)
-
-    return lax.fori_loop(0, size, hop, start)
+def state_kernel(reverse, planes, f_ref, t_ref, o_ref, gath, tg, zin, zout, back, s_a, r_a, s_t, r_t, s_z, r_z, s_b, r_b):
+    me = lax.axis_index("dp")
+    i = lax.rem(me, PLANE)
+    q = me // PLANE
+    per = zin.shape[0]
+    at = planes - 1 - q if reverse else q
+    ahead = me - PLANE if reverse else me + PLANE
+    behind = me + PLANE if reverse else me - PLANE
+    order = tuple(reversed(range(PLANE))) if reverse else tuple(range(PLANE))
+
+    def send(src, dst, ss, rs, to):
+        return pltpu.make_async_remote_copy(
+            src_ref=src, dst_ref=dst, send_sem=ss, recv_sem=rs, device_id={"dp": to}, device_id_type=pl.DeviceIdType.MESH
+        )
+
+    barrier = pltpu.get_barrier_semaphore()
+    peers = [lax.rem(i + k, PLANE) for k in range(1, PLANE)]
+    for peer in peers:
+        pl.semaphore_signal(
+            barrier, inc=1, device_id={"dp": q * PLANE + peer}, device_id_type=pl.DeviceIdType.MESH
+        )
+
+    @pl.when(at > 0)
+    def _():
+        pl.semaphore_signal(barrier, inc=1, device_id={"dp": behind}, device_id_type=pl.DeviceIdType.MESH)
+
+    @pl.when(at < planes - 1)
+    def _():
+        pl.semaphore_signal(barrier, inc=1, device_id={"dp": ahead}, device_id_type=pl.DeviceIdType.MESH)
+
+    chain = jnp.where(at > 0, 1, 0) + jnp.where(at < planes - 1, 1, 0)
+    pl.semaphore_wait(barrier, PLANE - 1 + chain)
+
+    t_copies = [
+        send(t_ref.at[peer], tg.at[i], s_t.at[k], r_t.at[k], q * PLANE + peer) for k, peer in enumerate(peers)
+    ]
+    for copy in t_copies:
+        copy.start()
+    a_copies = [
+        [
+            send(f_ref.at[peer * per + r], gath.at[i, r], s_a.at[r, k], r_a.at[r, k], q * PLANE + peer)
+            for k, peer in enumerate(peers)
+        ]
+        for r in range(per)
+    ]
+    for row in a_copies:
+        for copy in row:
+            copy.start()
+    tg[i] = t_ref[i]
+    for r in range(per):
+        gath[i, r] = f_ref[i * per + r]
+    for copy in t_copies:
+        copy.wait_recv()
+    z_copies = [send(zout.at[r], zin.at[r], s_z.at[r], r_z.at[r], ahead) for r in range(per)]
+    b_copies = []
+    for r in range(per):
+        for copy in a_copies[r]:
+            copy.wait_recv()
+
+        @pl.when(at == 0)
+        def _(r=r):
+            zin[r] = jnp.zeros_like(zin[r])
+
+        through = [tg[j, pl.ds(r, 1), :] for j in order]
+        states = [gath[j, r] for j in order]
+        total = states[0]
+        decay = through[0]
+        for j in range(1, PLANE):
+            total = states[j] + through[j] * total
+            decay = decay * through[j]
+
+        @pl.when(at > 0)
+        def _(r=r):
+            z_copies[r].wait_recv()
+
+        inc = zin[r]
+        zout[r] = total + decay * inc
+
+        @pl.when(at < planes - 1)
+        def _(r=r):
+            z_copies[r].start()
+
+        for j in range(PLANE):
+            back[order[j], r] = inc
+            inc = states[j] + through[j] * inc
+        o_ref[i * per + r] = back[i, r]
+        row = [
+            send(back.at[peer, r], o_ref.at[i * per + r], s_b.at[r, k], r_b.at[r, k], q * PLANE + peer)
+            for k, peer in enumerate(peers)
+        ]
+        for copy in row:
+            copy.start()
+        b_copies.append(row)
+    for copy in t_copies:
+        copy.wait_send()
+    for r in range(per):
+        for copy in a_copies[r]:
+            copy.wait_send()
+        for copy in b_copies[r]:
+            copy.wait()
+
+        @pl.when(at < planes - 1)
+        def _(r=r):
+            z_copies[r].wait_send()
+
+
+def entering(through, state, reverse, call):
+    heads, width, depth = state.shape
+    planes = lax.axis_size("dp") // PLANE
+    per = heads // PLANE
+    rows = -(-per // 8) * 8
+    spread = jnp.pad(through.reshape(PLANE, per), ((0, 0), (0, rows - per)))
+    spread = jnp.broadcast_to(spread[:, :, None], (PLANE, rows, depth))
+    f32 = jnp.float32
+    dma = pltpu.SemaphoreType.DMA
+    vmem = pl.BlockSpec(memory_space=pltpu.VMEM)
+    return pl.pallas_call(
+        functools.partial(state_kernel, reverse, planes),
+        out_shape=jax.ShapeDtypeStruct(state.shape, f32),
+        in_specs=[vmem, vmem],
+        out_specs=vmem,
+        scratch_shapes=[
+            pltpu.VMEM((PLANE, per, width, depth), f32),
+            pltpu.VMEM((PLANE, rows, depth), f32),
+            pltpu.VMEM((per, width, depth), f32),
+            pltpu.VMEM((per, width, depth), f32),
+            pltpu.VMEM((PLANE, per, width, depth), f32),
+            dma((per, PLANE - 1)),
+            dma((per, PLANE - 1)),
+            dma((PLANE - 1,)),
+            dma((PLANE - 1,)),
+            dma((per,)),
+            dma((per,)),
+            dma((per, PLANE - 1)),
+            dma((per, PLANE - 1)),
+        ],
+        compiler_params=pltpu.CompilerParams(collective_id=call, has_side_effects=True),
+        name="state_chain",
+    )(state, spread)
 
 
 def segment_of(positions, seq_ends):
@@ -133,13 +261,9 @@
     )
 
 
-def chain(earlier, later):
-    return (earlier[0] * later[0], later[0][:, None, None] * earlier[1] + later[1])
-
-
 def contract_rows(left, right):
     return lax.dot_general(
-        left, right, (((0,), (0,)), ((), ())), preferred_element_type=jnp.float32
+        left.astype(jnp.bfloat16), right.astype(jnp.bfloat16), (((0,), (0,)), ((), ())), preferred_element_type=jnp.float32
     )
 
 
@@ -147,6 +271,56 @@
     return lax.dot_general(
         left, right, (((1,), (1,)), ((), ())), preferred_element_type=jnp.float32
     )
+
+
+def swapped(array):
+    return lax.ppermute(array, "tensor", [(0, 1), (1, 0)])
+
+
+def pair_sum(array):
+    return array + swapped(array)
+
+
+def from_plane(array, k):
+    size = lax.axis_size("dp")
+    return lax.ppermute(array, "dp", [(d, d ^ k) for d in range(size)])
+
+
+def plane_gather(rows):
+    core = lax.axis_index("tensor")
+    half = rows.shape[1] // 2
+    mine = lax.dynamic_slice_in_dim(rows, core * half, half, 1)
+    mine = jnp.concatenate([mine] + [from_plane(mine, k) for k in range(1, PLANE)], 0)
+    other = swapped(mine)
+    first = jnp.where(core == 0, mine, other)
+    second = jnp.where(core == 0, other, mine)
+    return jnp.concatenate([first, second], 1)
+
+
+def plane_exchange(parts):
+    place = lax.rem(lax.axis_index("dp"), PLANE)
+    take = lambda k: lax.dynamic_index_in_dim(parts, place ^ k, 0, keepdims=False)
+    return jnp.concatenate([take(0)] + [from_plane(take(k), k) for k in range(1, PLANE)], 0)
+
+
+def columns_of(array, pad=0):
+    rows, columns = array.shape
+    parts = array.reshape(rows, PLANE, columns // PLANE).transpose(1, 0, 2)
+    return jnp.pad(parts, ((0, 0), (0, 0), (0, pad)))
+
+
+def plane_sums(all_left, all_right, unit):
+    size = lax.axis_size("dp")
+    part = contract_rows(all_left * unit, all_right * unit)
+    groups = [[q * PLANE + i for q in range(size // PLANE)] for i in range(PLANE)]
+    return lax.psum_scatter(part, "dp", scatter_dimension=0, axis_index_groups=groups, tiled=True)
+
+
+def hand_back(sums):
+    place = lax.rem(lax.axis_index("dp"), PLANE)
+    rows = sums.shape[0] // PLANE
+    got = plane_exchange(sums.reshape(PLANE, rows, -1)).reshape(PLANE, rows, -1)
+    return jnp.stack([lax.dynamic_index_in_dim(got, place ^ k, 0, keepdims=False) for k in range(PLANE)], 0)
 
 
 def per_device(
@@ -166,6 +340,7 @@
     token_rows = block_input.shape[0]
     inner_local = out_weight.shape[1]
     heads_local = head_params.shape[2]
+    bc_columns = bc_weight.shape[2]
     tail_rows = CONV - 1
     split_at = token_rows - tail_rows
     seq_ends = jnp.cumsum(seq_lengths)
@@ -176,6 +351,7 @@
         first_pos + jnp.arange(token_rows // GROUP, dtype=jnp.int32) * GROUP - 1, seq_ends
     )
     seg_prior = seg_before[0]
+    unit = (seq_lengths[0] > 0).astype(jnp.float32)
     alive_rows = (segments == seg_prior).astype(jnp.float32)
 
     def section_fn(x_act, dt_raw, bc_act, params):
@@ -193,6 +369,7 @@
         w_zx = zx_weight[layer_index].reshape(D, 2 * inner_local)
         normed_f, pull_norm = jax.vjp(rms_scale, hidden, norm_gain[layer_index])
         normed_bf = normed_f.astype(jnp.bfloat16)
+        normed_all = plane_gather(normed_f)
         projected = jnp.dot(normed_bf, w_zx, preferred_element_type=jnp.float32)
         gate_in = projected[:, :inner_local]
         x_pre = projected[:, inner_local:]
@@ -207,32 +384,25 @@
             section_fn, x_act, dt_raw, bc_act, head_params[layer_index]
         )
         outputs, final_state, through, cumulative, c_matrix = section_out
-        prefix = entering(
-            (through, final_state),
-            "dp",
-            chain,
-            (jnp.ones_like(through), jnp.zeros_like(final_state)),
-            False,
-        )
-        incoming = prefix[1]
+        incoming = entering(through, final_state, False, layer_index)
         from_state, pull_state = jax.vjp(state_fn, incoming, cumulative, c_matrix)
         ssd_out = (outputs + from_state).reshape(token_rows, inner_local)
         gated = ssd_out * jax.nn.silu(gate_in)
-        squares = lax.psum(jnp.sum(gated * gated, axis=1), "tensor")
+        squares = pair_sum(jnp.sum(gated * gated, axis=1))
         scale = lax.rsqrt(squares / INNER + epsilon)
-        mixed = (gated * scale[:, None] * gate_gain[layer_index]).astype(jnp.bfloat16)
-        out_sum = lax.psum(
-            jnp.dot(mixed, out_weight[layer_index], preferred_element_type=jnp.float32), "tensor"
-        )
+        mixed_f = gated * scale[:, None] * gate_gain[layer_index]
+        mixed = mixed_f.astype(jnp.bfloat16)
+        mixed_parts = plane_exchange(columns_of(mixed_f))
+        out_sum = pair_sum(jnp.dot(mixed, out_weight[layer_index], preferred_element_type=jnp.float32))
         kept.append(
             (
                 pull_norm,
-                normed_bf,
+                normed_all,
                 gate_in,
                 ssd_out,
                 gated,
                 scale,
-                mixed,
+                mixed_parts,
                 pull_cx,
                 pull_cbc,
                 pull_section,
@@ -249,12 +419,12 @@
     for layer_index in reversed(range(LAYERS)):
         (
             pull_norm,
-            normed_bf,
+            normed_all,
             gate_in,
             ssd_out,
             gated,
             scale,
-            mixed,
+            mixed_parts,
             pull_cx,
             pull_cbc,
             pull_section,
@@ -263,11 +433,12 @@
             through,
         ) = kept[layer_index]
         grad_bf = grad.astype(jnp.bfloat16)
-        d_out_w = contract_rows(mixed, grad_bf)
+        grad_all = plane_gather(grad)
+        d_out_w = plane_sums(grad_all, mixed_parts, unit)
         d_mixed = contract_cols(grad_bf, out_weight[layer_index])
         gain_row = gate_gain[layer_index]
         d_gate_gain = jnp.sum(d_mixed * gated * scale[:, None], axis=0)
-        dotted = lax.psum(jnp.sum(d_mixed * gain_row * gated, axis=1), "tensor")
+        dotted = pair_sum(jnp.sum(d_mixed * gain_row * gated, axis=1))
         d_gated = (
             scale[:, None] * gain_row * d_mixed
             - gated * (scale * scale * scale * dotted / INNER)[:, None]
@@ -277,19 +448,12 @@
         d_z = d_gated * ssd_out * sigma * (1.0 + gate_in * (1.0 - sigma))
         d_heads = d_ssd.reshape(token_rows, heads_local, -1)
         d_incoming, d_cumul, d_cmatrix = pull_state(d_heads)
-        later = entering(
-            (through, d_incoming),
-            "dp",
-            chain,
-            (jnp.ones_like(through), jnp.zeros_like(d_incoming)),
-            True,
-        )
-        d_final = later[1]
+        d_final = entering(through, d_incoming, True, LAYERS + layer_index)
         d_through = jnp.sum(d_final * incoming, axis=(1, 2))
         d_xact, d_dtraw, d_bcact, d_params = pull_section(
             (d_heads, d_final, d_through, d_cumul, d_cmatrix)
         )
-        d_bcact = lax.psum(d_bcact, "tensor")
+        d_bcact = pair_sum(d_bcact)
         d_xext, d_cx = pull_cx(d_xact)
         d_bcext, d_cbc = pull_cbc(d_bcact)
         back = shifted((d_xext[:tail_rows], d_bcext[:tail_rows]), "dp", -1)
@@ -297,30 +461,48 @@
         d_bccore = d_bcext[tail_rows:]
         d_xpre = jnp.concatenate([d_xcore[:split_at], d_xcore[split_at:] + back[0]], 0)
         d_bcpre = jnp.concatenate([d_bccore[:split_at], d_bccore[split_at:] + back[1]], 0)
-        d_proj = jnp.concatenate([d_z, d_xpre], 1).astype(jnp.bfloat16)
+        d_proj_f = jnp.concatenate([d_z, d_xpre], 1)
+        d_proj = d_proj_f.astype(jnp.bfloat16)
         d_bc_bf = d_bcpre.astype(jnp.bfloat16)
         d_dt_bf = d_dtraw.astype(jnp.bfloat16)
         w_zx = zx_weight[layer_index].reshape(D, 2 * inner_local)
-        d_zx_w = contract_rows(normed_bf, d_proj).reshape(D, 2, inner_local)
-        d_bc_w = contract_rows(normed_bf, d_bc_bf)
-        d_dt_w = contract_rows(normed_bf, d_dt_bf)
+        small_pad = -(bc_columns + heads_local) // PLANE % 128
+        parts = jnp.concatenate(
+            [
+                columns_of(d_proj_f),
+                columns_of(d_bcpre),
+                columns_of(d_dtraw, small_pad),
+            ],
+            2,
+        )
+        d_in_w = plane_sums(normed_all, plane_exchange(parts), unit)
         head_part = contract_cols(d_proj, w_zx) + contract_cols(d_dt_bf, dt_weight[layer_index])
-        d_normed = lax.psum(head_part, "tensor") + contract_cols(d_bc_bf, bc_weight[layer_index])
+        d_normed = pair_sum(head_part) + contract_cols(d_bc_bf, bc_weight[layer_index])
         d_hidden, d_norm_gain = pull_norm(d_normed)
         grad = grad + d_hidden
-        large_list.insert(0, (d_zx_w, d_bc_w, d_dt_w, d_out_w))
+        large_list.insert(0, (d_in_w, d_out_w))
         small_list.insert(0, (d_norm_gain, d_cx, d_cbc, d_params, d_gate_gain))
-    large_stack = tuple((jnp.stack([entry[slot] for entry in large_list], 0) for slot in range(4)))
+
+    def join(parts):
+        return parts.transpose(1, 0, 2).reshape(parts.shape[1], -1)
+
+    grads = []
+    for d_in_w, d_out_w in large_list:
+        got = hand_back(jnp.concatenate([d_in_w, d_out_w], 1))
+        zx_end = 2 * inner_local // PLANE
+        bc_end = zx_end + bc_columns // PLANE
+        dt_end = bc_end + heads_local // PLANE
+        grads.append(
+            (
+                join(got[:, :, :zx_end]).reshape(-1, 2, inner_local),
+                join(got[:, :, zx_end:bc_end]),
+                join(got[:, :, bc_end:dt_end]),
+                join(got[:, :, d_in_w.shape[1] :]).T,
+            )
+        )
+    large_sums = tuple(jnp.stack([entry[slot] for entry in grads], 0) for slot in range(4))
     small_stack = tuple((jnp.stack([entry[slot] for entry in small_list], 0) for slot in range(5)))
-    large_sums = (
-        lax.psum_scatter(large_stack[0], "dp", scatter_dimension=1, tiled=True),
-        lax.psum_scatter(large_stack[1], "dp", scatter_dimension=1, tiled=True),
-        lax.psum_scatter(large_stack[2], "dp", scatter_dimension=1, tiled=True),
-        lax.psum_scatter(large_stack[3], "dp", scatter_dimension=2, tiled=True),
-    )
-    small_sums = lax.psum(
-        (small_stack[0], small_stack[1], small_stack[2], small_stack[3], small_stack[4]), "dp"
-    )
+    small_sums = lax.psum(small_stack, "dp")
     return (
         block_output,
         grad,

time: 2570 us -> 955 us (0.37)
  waiting for transfers between devices: 1760 us -> 234 us
  Pallas kernels: 0 us -> 137 us
  local copies, waits for them, and re-layouts: 274 us -> 170 us
  blocking collectives: 92.4 us -> 0 us
  other arithmetic: 209 us -> 145 us
  starting transfers between devices: 22.3 us -> 65.7 us
    unnamed x15 -> x5, waiting for transfers between devices: 1000 us -> 0.08 us
    all_gather x4 -> x0, waiting for transfers between devices: 476 us -> none  [entering(): everything = jax.tree.map(lambda part: lax.all_gather(part, axis), array)]
    pallas_call x0 -> x4, Pallas kernels: none -> 137 us  [entering(): pl.pallas_call(functools.partial(state_kernel, reverse, planes), out_shap...]
    reduce_scatter x1 -> x4, waiting for transfers between devices: 131 us -> 0.03 us  [plane_sums(): lax.psum_scatter(part, 'dp', scatter_dimension=0, axis_index_groups=group...]
    ppermute x0 -> x44, waiting for transfers between devices: none -> 111 us  [the longest x30 111 us: from_plane(): return lax.ppermute(array, 'dp', [(d, d ^ k) for d in range(size)])]
    all_gather x2 -> x0, blocking collectives: 82.2 us -> none  [entering(): everything = jax.tree.map(lambda part: lax.all_gather(part, axis), array)]
    select_n x64 -> x4, other arithmetic: 83.1 us -> 12.9 us  [plane_gather(): first = jnp.where(core == 0, mine, other)]
    another operation x21 -> x24, local copies, waits for them, and re-layouts: 78.8 us -> 18.1 us  [the longest x3 78 us: per_device(): jnp.stack([entry[slot] for entry in large_list], 0)]
  transfers between devices with their start and end apart: 20 -> 57, of which waited for: 16 -> 16; matrix products, arithmetic and copies ran while one was open for 13% -> 41% of each run, Pallas kernels for 0% -> 12%
where the time goes in v1:
time: 955 us; the launch traced here: 944 us
  waiting for transfers between devices  234 us (25%)
  matrix products  172 us (18%)
  local copies, waits for them, and re-layouts  170 us (18%)
  other arithmetic  145 us (15%)
  Pallas kernels  137 us (14%)
  starting transfers between devices  65.7 us (7%)
  between operations  20.3 us (2%)
    pallas_call x4, Pallas kernels, entering(): pl.pallas_call(functools.partial(state_kernel, reverse, planes), out_shap...  137 us
    psum x1, waiting for transfers between devices, per_device(): small_sums = lax.psum(small_stack, 'dp')  115 us
    ppermute x30, waiting for transfers between devices, from_plane(): return lax.ppermute(array, 'dp', [(d, d ^ k) for d in range(size)])  111 us
    unnamed x506, local copies, waits for them, and re-layouts  57.9 us
    dot_general x6, matrix products, group_step(): jnp.einsum('ijh,jhp->ihp', decayed * intersection[:, :, None], x_scaled,...  53.2 us
    ppermute x30, starting transfers between devices, from_plane(): return lax.ppermute(array, 'dp', [(d, d ^ k) for d in range(size)])  41.5 us
    dot_general x8, matrix products, contract_cols(): lax.dot_general(left, right, (((1,), (1,)), ((), ())), preferred_element_...  26.5 us
    dot_general x4, matrix products, contract_rows(): lax.dot_general(left.astype(jnp.bfloat16), right.astype(jnp.bfloat16), ((...  21.4 us
  transfers between devices with their start and end apart: 57, of which 16 were waited for; matrix products, arithmetic and copies ran while one was open for 41% of the time, Pallas kernels for 12%

profile of v1, /device:TPU:0, one launch (start us, length us, event | category | flops | bytes accessed | tf_op | source)
XLA Modules:
  0.0 944.2 jit_solution(18030643634664781549)
XLA Ops:
  8.1 15.8 %fusion.339 = (bf16[1,1536,2,1536]{3,2,1,0:T(2,128)(2,1)}, bf16[1,1536,2,1536]{3,2,1,0:T(2,128)(2,1)}) fusion(bf16[2,1536,2,1536]{3,2,1,0:T(2,128)(2,1)} %param.15), kind=kLoop, calls=%fused_computation.629 | loop fusion | bytes 37748736 | tf_op jit(solution)/shard_map/slice | solution.py:369
  23.9 9.9 %copy.236 = bf16[192,8,2,1536]{3,1,2,0:T(8,128)(2,1)} copy(bf16[192,8,2,1536]{3,2,1,0:T(2,128)(2,1)} %bitcast.516) | data formatting | bytes 18874368
  34.2 5.3 fusion.322
  41.2 5.0 collective-permute-start
  73.2 23.4 %state_chain.4 = f32[24,64,128]{2,1,0:T(8,128)} custom-call(f32[24,64,128]{2,1,0:T(8,128)} %fusion.143.f_ref, f32[4,8,128]{2,1,0:T(8,128)} %broadcast_in_dim.434.t_ref), custom_call_target="tpu_custom_call" | custom-call | tf_op jit(solution)/shard_map/state_chain/pallas_call | solution.py:143
  99.3 8.2 fusion.100
  113.8 4.9 fusion.26
  125.8 9.8 %copy.237 = bf16[192,8,2,1536]{3,1,2,0:T(8,128)(2,1)} copy(bf16[192,8,2,1536]{3,2,1,0:T(2,128)(2,1)} %bitcast.515) | data formatting | bytes 18874368
  137.4 5.1 constant_dynamic-slice_fusion.21
  191.2 24.5 %state_chain.5 = f32[24,64,128]{2,1,0:T(8,128)} custom-call(f32[24,64,128]{2,1,0:T(8,128)} %fusion.146.f_ref, f32[4,8,128]{2,1,0:T(8,128)} %broadcast_in_dim.435.t_ref), custom_call_target="tpu_custom_call" | custom-call | tf_op jit(solution)/shard_map/state_chain/pallas_call | solution.py:143
  218.6 10.1 %fusion.98 = f32[256,24,64]{0,2,1:T(8,128)} fusion(f32[256,24,64]{0,2,1:T(8,128)S(1)} %fusion.235, f32[256,24,64]{0,2,1:T(8,128)S(1)} %bitcast.524, f32[256,24,64]{0,2,1:T(8,128)} %fusion.210, f32[256,256]{1,0:T(8,128)S(1)} %copy-done.95, f32[256,24]{0,1:T(8,128)S(1)} %copy-done.111, pred[256,256]{1,0:T(8,128)(4,1)S(1)} %copy-done.157, ...), kind=kOutput, calls=%fused_computation.140 | convolution fusion | flops 1215430656 | bytes 6692960 | tf_op jit(solution)/shard_map/jvp()/while/body/eval_jaxpr/ijh,jhp->ihp/dot_general | solution.py:200
  262.7 49.8 %state_chain.6 = f32[24,64,128]{2,1,0:T(8,128)} custom-call(f32[24,64,128]{2,1,0:T(8,128)} %fusion.141.f_ref, f32[4,8,128]{2,1,0:T(8,128)} %broadcast_in_dim.435.t_ref), custom_call_target="tpu_custom_call" | custom-call | tf_op jit(solution)/shard_map/state_chain/pallas_call | solution.py:143
  312.5 5.0 fusion.164
  321.3 9.6 %fusion.33 = (f32[256,24]{0,1:T(8,128)}, f32[256,24]{0,1:T(8,128)}, f32[256,256]{1,0:T(8,128)}) fusion(f32[256,256]{1,0:T(8,128)S(1)} %copy-done.96, f32[256,24]{0,1:T(8,128)S(1)} %copy-done.112, pred[256,256]{1,0:T(8,128)(4,1)S(1)} %copy-done.158, f32[24,64,256]{2,1,0:T(8,128)S(1)} %bitcast.512, f32[256,24,64]{0,2,1:T(8,128)S(1)} %bitcast.525, ...), kind=kOutput, calls=%fused_computation.39 | convolution fusion | flops 1222430720 | bytes 3833856 | tf_op jit(solution)/shard_map/transpose(jvp())/while/body/eval_jaxpr/ijh,jhp->ihp/dot_general | solution.py:200
  330.9 7.3 multiply_reduce_fusion.1
  408.8 7.5 convolution_add_fusion.1
  416.4 5.2 reshape.862
  444.6 6.7 collective-permute-done.35
  471.1 6.7 collective-permute-done.47
  500.6 39.5 %state_chain.7 = f32[24,64,128]{2,1,0:T(8,128)} custom-call(f32[24,64,128]{2,1,0:T(8,128)} %fusion.135.f_ref, f32[4,8,128]{2,1,0:T(8,128)} %broadcast_in_dim.434.t_ref), custom_call_target="tpu_custom_call" | custom-call | tf_op jit(solution)/shard_map/state_chain/pallas_call | solution.py:143
  553.0 7.7 fusion.40
  562.1 8.4 multiply_reduce_fusion
  576.1 9.6 %fusion.35 = (f32[256,24]{0,1:T(8,128)S(1)}, f32[256,24]{0,1:T(8,128)S(1)}, f32[256,256]{1,0:T(8,128)}) fusion(f32[256,256]{1,0:T(8,128)S(1)} %copy-done.94, f32[256,24]{0,1:T(8,128)S(1)} %copy-done.109, pred[256,256]{1,0:T(8,128)(4,1)S(1)} %copy-done.159, f32[24,64,256]{2,1,0:T(8,128)S(1)} %bitcast.505, f32[256,24,64]{0,2,1:T(8,128)S(1)} %bitcast.520, ...), kind=kOutput, calls=%fused_computation.41 | convolution fusion | flops 1222430720 | bytes 3833856 | tf_op jit(solution)/shard_map/transpose(jvp())/while/body/eval_jaxpr/ijh,jhp->ihp/dot_general | solution.py:200
  626.2 13.5 %collective-permute-done.25 = f32[256,768]{1,0:T(8,128)S(1)} collective-permute-done((f32[256,768]{1,0:T(8,128)}, f32[256,768]{1,0:T(8,128)S(1)}, u32[]{:S(2)}, u32[]{:S(2)}) %collective-permute-start.25) | collective-permute-done | bytes 786464 | tf_op jit(solution)/shard_map/ppermute | solution.py:286
  672.3 13.6 %collective-permute-done.20 = f32[256,768]{1,0:T(8,128)} collective-permute-done((f32[256,768]{1,0:T(8,128)}, f32[256,768]{1,0:T(8,128)}, u32[]{:S(2)}, u32[]{:S(2)}) %collective-permute-start.20) | collective-permute-done | bytes 786464 | tf_op jit(solution)/shard_map/ppermute | solution.py:286
  685.9 12.0 %collective-permute-done.19 = f32[256,768]{1,0:T(8,128)} collective-permute-done((f32[256,768]{1,0:T(8,128)}, f32[256,768]{1,0:T(8,128)}, u32[]{:S(2)}, u32[]{:S(2)}) %collective-permute-start.19) | collective-permute-done | bytes 786464 | tf_op jit(solution)/shard_map/ppermute | solution.py:286
  721.6 17.1 %collective-permute-done.24 = f32[256,896]{1,0:T(8,128)S(1)} collective-permute-done((f32[256,896]{1,0:T(8,128)S(1)}, f32[256,896]{1,0:T(8,128)S(1)}, u32[]{:S(2)}, u32[]{:S(2)}) %collective-permute-start.24) | collective-permute-done | bytes 917536 | tf_op jit(solution)/shard_map/ppermute | solution.py:286
  738.6 19.3 %collective-permute-done.23 = f32[256,896]{1,0:T(8,128)S(1)} collective-permute-done((f32[256,896]{1,0:T(8,128)S(1)}, f32[256,896]{1,0:T(8,128)S(1)}, u32[]{:S(2)}, u32[]{:S(2)}) %collective-permute-start.23) | collective-permute-done | bytes 917536 | tf_op jit(solution)/shard_map/ppermute | solution.py:286
  758.3 5.9 fusion.44
  772.0 115.1 %all-reduce.61.cloned.1.call-done = (f32[2,1536]{1,0:T(2,128)}, f32[2,5,1536]{2,1,0:T(8,128)}, f32[2,5,256]{2,1,0:T(8,128)}, f32[2,3,24]{2,1,0:T(4,128)}, f32[2,1536]{1,0:T(2,128)}) async-done(((f32[2,1536]{1,0:T(2,128)}, f32[2,5,1536]{2,1,0:T(8,128)}, f32[2,5,256]{2,1,0:T(8,128)}, f32[2,3,24]{2,1,0:T(4,128)}, f32[2,1536]{1,0:T(2,128)}), (f32[2,1536]{1,0:T(2,128)}, f32[2,5,1536]{2,1,0:T(8,128)}, ...) | async-done | bytes 96848 | tf_op jit(solution)/shard_map/psum | solution.py:505
  904.1 7.2 collective-permute-done.34
  911.3 7.6 collective-permute-done.33
  (892 shorter events, 427.4 us)
Async XLA Ops:
  8.0 756.9 %reduce-scatter.11.cloned.1.call-start = ((), (), s32[]{:S(2)}) async-start(), calls=%async_computation.7 | async-start | bytes 2949120 | tf_op jit(solution)/shard_map/reduce_scatter | solution.py:316
  118.7 26.9 %collective-permute-start.3 = (f32[256,1536]{1,0:T(8,128)}, f32[256,1536]{1,0:T(8,128)}, u32[]{:S(2)}, u32[]{:S(2)}) collective-permute-start(f32[256,1536]{1,0:T(8,128)} %fusion.26), channel_id=1, source_target_pairs={{0,1},{1,0},{2,3},{3,2},{4,5},{5,4},{6,7},{7,6},{8,9},{9,8},{10,11... | collective-permute-start | bytes 4718600 | tf_op jit(solution)/shard_map/ppermute | solution.py:277
  122.3 111.9 %collective-permute-start.44 = (f32[256,768]{1,0:T(8,128)}, f32[256,768]{1,0:T(8,128)}, u32[]{:S(2)}, u32[]{:S(2)}) collective-permute-start(f32[256,768]{1,0:T(8,128)} %constant_dynamic-slice_fusion.8), channel_id=1, source_target_pairs={{0,6},{2,4},{4,2},{6,0},{8,14},{10,12},{12,10},{14,8},{16,22},{18,... | collective-permute-start | bytes 2359304 | tf_op jit(solution)/shard_map/ppermute | solution.py:286
  124.1 110.2 %collective-permute-start.43 = (f32[256,768]{1,0:T(8,128)}, f32[256,768]{1,0:T(8,128)}, u32[]{:S(2)}, u32[]{:S(2)}) collective-permute-start(f32[256,768]{1,0:T(8,128)} %constant_dynamic-slice_fusion.8), channel_id=1, source_target_pairs={{0,4},{2,6},{4,0},{6,2},{8,12},{10,14},{12,8},{14,10},{16,20},{18,... | collective-permute-start | bytes 2359304 | tf_op jit(solution)/shard_map/ppermute | solution.py:286
  124.7 109.6 %collective-permute-start.42 = (f32[256,768]{1,0:T(8,128)}, f32[256,768]{1,0:T(8,128)}, u32[]{:S(2)}, u32[]{:S(2)}) collective-permute-start(f32[256,768]{1,0:T(8,128)} %constant_dynamic-slice_fusion.8), channel_id=1, source_target_pairs={{0,2},{2,0},{4,6},{6,4},{8,10},{10,8},{12,14},{14,12},{16,18},{18,... | collective-permute-start | bytes 2359304 | tf_op jit(solution)/shard_map/ppermute | solution.py:286
  238.1 222.9 %collective-permute-start.45 = (f32[1024,768]{1,0:T(8,128)}, f32[1024,768]{1,0:T(8,128)}, u32[]{:S(2)}, u32[]{:S(2)}) collective-permute-start(f32[1024,768]{1,0:T(8,128)} %pad_maximum_fusion.3), channel_id=1, source_target_pairs={{0,1},{1,0},{2,3},{3,2},{4,5},{5,4},{6,7},{7,6},{8,9},{9,8},{10,11... | collective-permute-start | bytes 9437192 | tf_op jit(solution)/shard_map/ppermute | solution.py:277
  243.8 199.6 %collective-permute-start.37 = (f32[256,768]{1,0:T(8,128)}, f32[256,768]{1,0:T(8,128)}, u32[]{:S(2)}, u32[]{:S(2)}) collective-permute-start(f32[256,768]{1,0:T(8,128)} %constant_dynamic-slice_fusion.13), channel_id=1, source_target_pairs={{0,6},{2,4},{4,2},{6,0},{8,14},{10,12},{12,10},{14,8},{16,22},{18,... | collective-permute-start | bytes 2359304 | tf_op jit(solution)/shard_map/ppermute | solution.py:286
  244.6 200.1 %collective-permute-start.36 = (f32[256,768]{1,0:T(8,128)}, f32[256,768]{1,0:T(8,128)}, u32[]{:S(2)}, u32[]{:S(2)}) collective-permute-start(f32[256,768]{1,0:T(8,128)} %constant_dynamic-slice_fusion.13), channel_id=1, source_target_pairs={{0,4},{2,6},{4,0},{6,2},{8,12},{10,14},{12,8},{14,10},{16,20},{18,... | collective-permute-start | bytes 2359304 | tf_op jit(solution)/shard_map/ppermute | solution.py:286
  394.4 27.7 %collective-permute-start.11 = (f32[256,256]{1,0:T(8,128)}, f32[256,256]{1,0:T(8,128)}, u32[]{:S(2)}, u32[]{:S(2)}) collective-permute-start(f32[256,256]{1,0:T(8,128)} %pad_add_fusion.5), channel_id=1, source_target_pairs={{0,1},{1,0},{2,3},{3,2},{4,5},{5,4},{6,7},{7,6},{8,9},{9,8},{10,11... | collective-permute-start | bytes 786440 | tf_op jit(solution)/shard_map/ppermute | solution.py:277
  421.6 36.9 %collective-permute-start.10 = (f32[256,1536]{1,0:T(8,128)}, f32[256,1536]{1,0:T(8,128)}, u32[]{:S(2)}, u32[]{:S(2)}) collective-permute-start(f32[256,1536]{1,0:T(8,128)} %convolution_add_fusion.1), channel_id=1, source_target_pairs={{0,1},{1,0},{2,3},{3,2},{4,5},{5,4},{6,7},{7,6},{8,9},{9,8},{10,11... | collective-permute-start | bytes 4718600 | tf_op jit(solution)/shard_map/ppermute | solution.py:277
  443.3 218.7 %collective-permute-start.31 = (f32[256,384]{1,0:T(8,128)}, f32[256,384]{1,0:T(8,128)}, u32[]{:S(2)}, u32[]{:S(2)}) collective-permute-start(f32[256,384]{1,0:T(8,128)} %bitcast.490), channel_id=1, source_target_pairs={{0,6},{2,4},{4,2},{6,0},{8,14},{10,12},{12,10},{14,8},{16,22},{18,... | collective-permute-start | bytes 1179656 | tf_op jit(solution)/shard_map/ppermute | solution.py:286
  444.6 36.9 %collective-permute-start.7 = (f32[256,1536]{1,0:T(8,128)}, f32[256,1536]{1,0:T(8,128)}, u32[]{:S(2)}, u32[]{:S(2)}) collective-permute-start(f32[256,1536]{1,0:T(8,128)} %fusion.22), channel_id=1, source_target_pairs={{0,1},{1,0},{2,3},{3,2},{4,5},{5,4},{6,7},{7,6},{8,9},{9,8},{10,11... | collective-permute-start | bytes 4718600 | tf_op jit(solution)/shard_map/ppermute | solution.py:277
  469.4 80.9 %collective-permute-start.41 = (f32[256,896]{1,0:T(8,128)}, f32[256,896]{1,0:T(8,128)}, u32[]{:S(2)}, u32[]{:S(2)}) collective-permute-start(f32[256,896]{1,0:T(8,128)} %bitcast.478), channel_id=1, source_target_pairs={{0,6},{2,4},{4,2},{6,0},{8,14},{10,12},{12,10},{14,8},{16,22},{18,... | collective-permute-start | bytes 2752520 | tf_op jit(solution)/shard_map/ppermute | solution.py:286
  477.8 74.4 %collective-permute-start.40 = (f32[256,896]{1,0:T(8,128)}, f32[256,896]{1,0:T(8,128)}, u32[]{:S(2)}, u32[]{:S(2)}) collective-permute-start(f32[256,896]{1,0:T(8,128)} %bitcast.479), channel_id=1, source_target_pairs={{0,4},{2,6},{4,0},{6,2},{8,12},{10,14},{12,8},{14,10},{16,20},{18,... | collective-permute-start | bytes 2752520 | tf_op jit(solution)/shard_map/ppermute | solution.py:286
  478.0 68.2 %collective-permute-start.38 = (f32[1024,768]{1,0:T(8,128)}, f32[1024,768]{1,0:T(8,128)}, u32[]{:S(2)}, u32[]{:S(2)}) collective-permute-start(f32[1024,768]{1,0:T(8,128)} %pad_maximum_fusion.2), channel_id=1, source_target_pairs={{0,1},{1,0},{2,3},{3,2},{4,5},{5,4},{6,7},{7,6},{8,9},{9,8},{10,11... | collective-permute-start | bytes 9437192 | tf_op jit(solution)/shard_map/ppermute | solution.py:277
  481.3 283.7 %reduce-scatter.9.cloned.1.call-start = ((), (), s32[]{:S(2)}) async-start(), calls=%async_computation.6 | async-start | bytes 6881280 | tf_op jit(solution)/shard_map/reduce_scatter | solution.py:316
  492.8 60.2 %collective-permute-start.39 = (f32[256,896]{1,0:T(8,128)}, f32[256,896]{1,0:T(8,128)}, u32[]{:S(2)}, u32[]{:S(2)}) collective-permute-start(f32[256,896]{1,0:T(8,128)} %bitcast.480), channel_id=1, source_target_pairs={{0,2},{2,0},{4,6},{6,4},{8,10},{10,8},{12,14},{14,12},{16,18},{18,... | collective-permute-start | bytes 2752520 | tf_op jit(solution)/shard_map/ppermute | solution.py:286
  546.2 121.6 %collective-permute-start.30 = (f32[256,384]{1,0:T(8,128)}, f32[256,384]{1,0:T(8,128)}, u32[]{:S(2)}, u32[]{:S(2)}) collective-permute-start(f32[256,384]{1,0:T(8,128)} %bitcast.555), channel_id=1, source_target_pairs={{0,4},{2,6},{4,0},{6,2},{8,12},{10,14},{12,8},{14,10},{16,20},{18,... | collective-permute-start | bytes 1179656 | tf_op jit(solution)/shard_map/ppermute | solution.py:286
  550.3 75.8 %collective-permute-start.27 = (f32[256,768]{1,0:T(8,128)}, f32[256,768]{1,0:T(8,128)}, u32[]{:S(2)}, u32[]{:S(2)}) collective-permute-start(f32[256,768]{1,0:T(8,128)} %constant_dynamic-slice_fusion.22), channel_id=1, source_target_pairs={{0,6},{2,4},{4,2},{6,0},{8,14},{10,12},{12,10},{14,8},{16,22},{18,... | collective-permute-start | bytes 2359304 | tf_op jit(solution)/shard_map/ppermute | solution.py:286
  552.1 74.1 %collective-permute-start.26 = (f32[256,768]{1,0:T(8,128)}, f32[256,768]{1,0:T(8,128)}, u32[]{:S(2)}, u32[]{:S(2)}) collective-permute-start(f32[256,768]{1,0:T(8,128)} %constant_dynamic-slice_fusion.22), channel_id=1, source_target_pairs={{0,4},{2,6},{4,0},{6,2},{8,12},{10,14},{12,8},{14,10},{16,20},{18,... | collective-permute-start | bytes 2359304 | tf_op jit(solution)/shard_map/ppermute | solution.py:286
  560.8 326.4 %all-reduce.61.cloned.1.call-start = ((), (), s32[]{:S(2)}) async-start(), calls=%async_computation.8 | async-start | bytes 286720 | tf_op jit(solution)/shard_map/psum | solution.py:505
  660.2 25.7 %collective-permute-start.20 = (f32[256,768]{1,0:T(8,128)}, f32[256,768]{1,0:T(8,128)}, u32[]{:S(2)}, u32[]{:S(2)}) collective-permute-start(f32[256,768]{1,0:T(8,128)} %constant_dynamic-slice_fusion.27), channel_id=1, source_target_pairs={{0,6},{2,4},{4,2},{6,0},{8,14},{10,12},{12,10},{14,8},{16,22},{18,... | collective-permute-start | bytes 2359304 | tf_op jit(solution)/shard_map/ppermute | solution.py:286
  661.9 231.0 %reduce-scatter.7.cloned.1.call-start = ((), (), s32[]{:S(2)}) async-start(), calls=%async_computation.5 | async-start | bytes 2949120 | tf_op jit(solution)/shard_map/reduce_scatter | solution.py:316
  662.0 35.9 %collective-permute-start.19 = (f32[256,768]{1,0:T(8,128)}, f32[256,768]{1,0:T(8,128)}, u32[]{:S(2)}, u32[]{:S(2)}) collective-permute-start(f32[256,768]{1,0:T(8,128)} %constant_dynamic-slice_fusion.27), channel_id=1, source_target_pairs={{0,4},{2,6},{4,0},{6,2},{8,12},{10,14},{12,8},{14,10},{16,20},{18,... | collective-permute-start | bytes 2359304 | tf_op jit(solution)/shard_map/ppermute | solution.py:286
  662.6 37.3 %collective-permute-start.18 = (f32[256,768]{1,0:T(8,128)}, f32[256,768]{1,0:T(8,128)}, u32[]{:S(2)}, u32[]{:S(2)}) collective-permute-start(f32[256,768]{1,0:T(8,128)} %constant_dynamic-slice_fusion.27), channel_id=1, source_target_pairs={{0,2},{2,0},{4,6},{6,4},{8,10},{10,8},{12,14},{14,12},{16,18},{18,... | collective-permute-start | bytes 2359304 | tf_op jit(solution)/shard_map/ppermute | solution.py:286
  672.3 220.7 %reduce-scatter.5.cloned.1.call-start = ((), (), s32[]{:S(2)}) async-start(), calls=%async_computation.4 | async-start | bytes 6881280 | tf_op jit(solution)/shard_map/reduce_scatter | solution.py:316
  714.4 24.2 %collective-permute-start.24 = (f32[256,896]{1,0:T(8,128)S(1)}, f32[256,896]{1,0:T(8,128)S(1)}, u32[]{:S(2)}, u32[]{:S(2)}) collective-permute-start(f32[256,896]{1,0:T(8,128)S(1)} %bitcast.548), channel_id=1, source_target_pairs={{0,6},{2,4},{4,2},{6,0},{8,14},{10,12},{12,10},{14,8},{16,22},{18,... | collective-permute-start | bytes 2752520 | tf_op jit(solution)/shard_map/ppermute | solution.py:286
  717.2 40.8 %collective-permute-start.23 = (f32[256,896]{1,0:T(8,128)S(1)}, f32[256,896]{1,0:T(8,128)S(1)}, u32[]{:S(2)}, u32[]{:S(2)}) collective-permute-start(f32[256,896]{1,0:T(8,128)S(1)} %bitcast.550), channel_id=1, source_target_pairs={{0,4},{2,6},{4,0},{6,2},{8,12},{10,14},{12,8},{14,10},{16,20},{18,... | collective-permute-start | bytes 2752520 | tf_op jit(solution)/shard_map/ppermute | solution.py:286
  717.6 40.7 %collective-permute-start.22 = (f32[256,896]{1,0:T(8,128)S(1)}, f32[256,896]{1,0:T(8,128)S(1)}, u32[]{:S(2)}, u32[]{:S(2)}) collective-permute-start(f32[256,896]{1,0:T(8,128)S(1)} %bitcast.551), channel_id=1, source_target_pairs={{0,2},{2,0},{4,6},{6,4},{8,10},{10,8},{12,14},{14,12},{16,18},{18,... | collective-permute-start | bytes 2752520 | tf_op jit(solution)/shard_map/ppermute | solution.py:286
  766.9 124.4 %collective-permute-start.51 = (f32[96,1280]{1,0:T(8,128)S(1)}, f32[96,1280]{1,0:T(8,128)S(1)}, u32[]{:S(2)}, u32[]{:S(2)}) collective-permute-start(f32[96,1280]{1,0:T(8,128)S(1)} %get-tuple-element.535), channel_id=1, source_target_pairs={{0,6},{2,4},{4,2},{6,0},{8,14},{10,12},{12,10},{14,8},{16,22},{18,... | collective-permute-start | bytes 1474568 | tf_op jit(solution)/shard_map/ppermute | solution.py:286
  768.5 122.8 %collective-permute-start.50 = (f32[96,1280]{1,0:T(8,128)S(1)}, f32[96,1280]{1,0:T(8,128)S(1)}, u32[]{:S(2)}, u32[]{:S(2)}) collective-permute-start(f32[96,1280]{1,0:T(8,128)S(1)} %get-tuple-element.536), channel_id=1, source_target_pairs={{0,4},{2,6},{4,0},{6,2},{8,12},{10,14},{12,8},{14,10},{16,20},{18,... | collective-permute-start | bytes 1474568 | tf_op jit(solution)/shard_map/ppermute | solution.py:286
  769.7 121.6 %collective-permute-start.49 = (f32[96,1280]{1,0:T(8,128)S(1)}, f32[96,1280]{1,0:T(8,128)S(1)}, u32[]{:S(2)}, u32[]{:S(2)}) collective-permute-start(f32[96,1280]{1,0:T(8,128)S(1)} %get-tuple-element.537), channel_id=1, source_target_pairs={{0,2},{2,0},{4,6},{6,4},{8,10},{10,8},{12,14},{14,12},{16,18},{18,... | collective-permute-start | bytes 1474568 | tf_op jit(solution)/shard_map/ppermute | solution.py:286
  (265 other events, 1986.5 us)
Sparse Core Ops, SparseCore 0:
  481.4 51.1 reduce-scatter.10
  560.9 95.8 reduce-scatter.8
  672.4 46.8 reduce-scatter.6
  764.4 95.5 reduce-scatter.4
Sparse Core Ops, SparseCore 1:
  662.0 225.0 all-reduce.60
